TPU v7x, 32 devices: a whole 2x2x4 slice. The times are simulated.
32 devices in a mesh: shard: 4 (over y, x), ctx: 8 (over z, core).
Axes of the slice: x: 2, y: 2, z: 4, core: 2. Of those that a mesh axis runs over, the one named last changes fastest.
Arguments:
- layer_input: bfloat16 [4, 1024, 768], P('shard', 'ctx'), may hold values from -6 to 6
- positions: int32 [4, 1024], P('shard', 'ctx'), may hold values from 0 to 1023, as said below
- cotangent: bfloat16 [4, 1024, 768], P('shard', 'ctx'), may hold values from -6 to 6
- ln1_gain: float32 [768], replicated, may hold values from 0.5 to 1.5
- ln1_bias: float32 [768], replicated, may hold values from -3 to 3
- ln2_gain: float32 [768], replicated, may hold values from 0.5 to 1.5
- ln2_bias: float32 [768], replicated, may hold values from -3 to 3
- w_qkv: bfloat16 [768, 2304], P('shard')
- qkv_bias: float32 [2304], replicated, may hold values from -3 to 3
- w_out: bfloat16 [768, 768], P('shard'), may hold values from -1.25 to 1.25
- w_up: bfloat16 [768, 3072], P('shard'), may hold values from -0.21875 to 0.21875
- up_bias: float32 [3072], replicated, may hold values from -3 to 3
- w_down: bfloat16 [3072, 768], P('shard'), may hold values from -0.109375 to 0.109375
Outputs:
- layer_output: bfloat16 [4, 1024, 768], P('shard', 'ctx')
- grad_input: bfloat16 [4, 1024, 768], P('shard', 'ctx')
- grad_ln1_gain: float32 [768], replicated
- grad_ln1_bias: float32 [768], replicated
- grad_ln2_gain: float32 [768], replicated
- grad_ln2_bias: float32 [768], replicated
- grad_w_qkv: float32 [768, 2304], P('shard')
- grad_qkv_bias: float32 [2304], replicated
- grad_w_out: float32 [768, 768], P('shard')
- grad_w_up: float32 [768, 3072], P('shard')
- grad_up_bias: float32 [3072], replicated
- grad_w_down: float32 [3072, 768], P('shard')
Inputs may be any that keep to these rules, and one draw needn't show every extreme that they name: In each sequence, the 128 tokens that one device holds along ctx carry consecutive positions starting at a multiple of 128; every position of the sequence occurs once.
All inputs are finite; a program needn't handle non-finite values.
Results may differ from a plain program's by a relative error of at most 0.018.
Values may be sent and summed in bfloat16 or wider, within the bound.
A program may use at most 128 MiB of HBM per device.

v0:
```python
import jax
import jax.numpy as jnp
from jax import lax
from jax.sharding import PartitionSpec as P

HEADS = 12
HEAD_DIM = 64
ROTARY = 16
EPSILON = 1e-05
NEGATIVE = -1e30


def shifted(shard, axis, by):
    count = lax.axis_size(axis)
    return lax.ppermute(shard, axis, [(i, (i + by) % count) for i in range(count)])


def layer_norm(values_in, gain_vec, bias_vec):
    centered = values_in - jnp.mean(values_in, axis=-1, keepdims=True)
    variance = jnp.mean(centered * centered, axis=-1, keepdims=True)
    return centered * lax.rsqrt(variance + EPSILON) * gain_vec + bias_vec


def rotary_tables(position_ids):
    half_dim = ROTARY // 2
    inverse_freq = 1.0 / 10000.0 ** (jnp.arange(half_dim, dtype=jnp.float32) * (2.0 / ROTARY))
    angles = position_ids.astype(jnp.float32)[..., None] * inverse_freq
    return (jnp.cos(angles), jnp.sin(angles))


def rotate(field_in, cosine, sine_table):
    half_dim = cosine.shape[-1]
    lead_part = field_in[..., :half_dim]
    second = field_in[..., half_dim : 2 * half_dim]
    remain = field_in[..., 2 * half_dim :]
    cos_wide = cosine[..., None, :]
    sin_wide = sine_table[..., None, :]
    return jnp.concatenate(
        [
            lead_part * cos_wide - second * sin_wide,
            second * cos_wide + lead_part * sin_wide,
            remain,
        ],
        axis=-1,
    )


def gelu_exact(field_in):
    return jax.nn.gelu(field_in, approximate=False)


def on_device(
    layer_input,
    positions,
    cotangent,
    ln1_gain,
    ln1_bias,
    ln2_gain,
    ln2_bias,
    w_qkv,
    qkv_bias,
    w_out,
    w_up,
    up_bias,
    w_down,
):
    seqs_here, block_len, feature_count = layer_input.shape
    row_count = seqs_here * block_len
    head_count = HEADS
    head_size = HEAD_DIM
    score_scale = head_size ** (-0.5)
    whole_qkv, whole_out, whole_up, whole_down = (
        lax.all_gather(w_qkv, "shard", axis=0, tiled=True),
        lax.all_gather(w_out, "shard", axis=0, tiled=True),
        lax.all_gather(w_up, "shard", axis=0, tiled=True),
        lax.all_gather(w_down, "shard", axis=0, tiled=True),
    )
    all_positions = lax.all_gather(positions, "ctx", axis=1, tiled=True)
    cycle_size = lax.axis_size("ctx")
    my_index = lax.axis_index("ctx")
    inputs = layer_input.astype(jnp.float32).reshape(row_count, feature_count)
    normed_one = layer_norm(inputs, ln1_gain, ln1_bias).astype(jnp.bfloat16)
    normed_two = layer_norm(inputs, ln2_gain, ln2_bias).astype(jnp.bfloat16)
    projected = jnp.dot(normed_one, whole_qkv, preferred_element_type=jnp.float32) + qkv_bias
    split_heads = projected.reshape(seqs_here, block_len, 3, head_count, head_size)
    cosine, sine_table = rotary_tables(positions)
    queries = rotate(split_heads[:, :, 0], cosine, sine_table).astype(jnp.bfloat16)
    key_rows = rotate(split_heads[:, :, 1], cosine, sine_table).astype(jnp.bfloat16)
    value_rows = split_heads[:, :, 2].astype(jnp.bfloat16)
    top_query = jnp.max(positions)

    def attend_block(running, key_blk, value_blk, key_pos):

        def attend_update(current):
            run_max, run_sum, run_acc = current
            scores = (
                jnp.einsum("sqhd,skhd->shqk", queries, key_blk, preferred_element_type=jnp.float32)
                * score_scale
            )
            allowed = key_pos[:, None, None, :] <= positions[:, None, :, None]
            masked = jnp.where(allowed, scores, NEGATIVE)
            new_max = jnp.maximum(run_max, jnp.max(masked, axis=-1))
            shrink = jnp.exp(run_max - new_max)
            weights_now = jnp.where(allowed, jnp.exp(masked - new_max[..., None]), 0.0)
            run_sum = run_sum * shrink + jnp.sum(weights_now, axis=-1)
            added_term = jnp.einsum(
                "shqk,skhd->sqhd",
                weights_now.astype(jnp.bfloat16),
                value_blk,
                preferred_element_type=jnp.float32,
            )
            run_acc = run_acc * jnp.transpose(shrink, (0, 2, 1))[..., None] + added_term
            return (new_max, run_sum, run_acc)

        return lax.cond(
            jnp.min(key_pos) <= top_query, attend_update, lambda unchanged: unchanged, running
        )

    initial = (
        jnp.full((seqs_here, head_count, block_len), NEGATIVE, jnp.float32),
        jnp.zeros((seqs_here, head_count, block_len), jnp.float32),
        jnp.zeros((seqs_here, block_len, head_count, head_size), jnp.float32),
    )
    own_block = attend_block(initial, key_rows, value_rows, positions)

    def cycle_forward(turn_index, carried):
        current, key_cur, value_cur = carried
        key_cur, value_cur = shifted((key_cur, value_cur), "ctx", 1)
        source = (my_index - turn_index) % cycle_size
        key_pos = lax.dynamic_slice_in_dim(all_positions, source * block_len, block_len, 1)
        return (attend_block(current, key_cur, value_cur, key_pos), key_cur, value_cur)

    (run_max, run_sum, run_acc), unused_key, unused_value = lax.fori_loop(
        1, cycle_size, cycle_forward, (own_block, key_rows, value_rows)
    )
    attn_vals = run_acc / jnp.transpose(run_sum, (0, 2, 1))[..., None]
    log_total = run_max + jnp.log(run_sum)
    attn_low = attn_vals.astype(jnp.bfloat16).reshape(row_count, feature_count)
    attn_branch = jnp.dot(attn_low, whole_out, preferred_element_type=jnp.float32)
    hidden_pre = jnp.dot(normed_two, whole_up, preferred_element_type=jnp.float32) + up_bias
    hidden_low = gelu_exact(hidden_pre).astype(jnp.bfloat16)
    mlp_branch = jnp.dot(hidden_low, whole_down, preferred_element_type=jnp.float32)
    layer_output = (
        (inputs + attn_branch + mlp_branch)
        .astype(jnp.bfloat16)
        .reshape(seqs_here, block_len, feature_count)
    )
    cot_low = cotangent.reshape(row_count, feature_count)
    cot_full = cot_low.astype(jnp.float32)
    grad_down = jnp.einsum("rf,rd->fd", hidden_low, cot_low, preferred_element_type=jnp.float32)
    grad_hidden = jnp.einsum("rd,fd->rf", cot_low, whole_down, preferred_element_type=jnp.float32)
    unused_gelu, gelu_back = jax.vjp(gelu_exact, hidden_pre)
    grad_pre = gelu_back(grad_hidden)[0].astype(jnp.bfloat16)
    grad_up_bias = jnp.sum(grad_pre.astype(jnp.float32), axis=0)
    grad_up = jnp.einsum("rd,rf->df", normed_two, grad_pre, preferred_element_type=jnp.float32)
    grad_two = jnp.einsum("rf,df->rd", grad_pre, whole_up, preferred_element_type=jnp.float32)
    grad_out = jnp.einsum("rd,re->de", attn_low, cot_low, preferred_element_type=jnp.float32)
    grad_attn = (
        jnp.einsum("re,de->rd", cot_low, whole_out, preferred_element_type=jnp.float32)
        .astype(jnp.bfloat16)
        .reshape(seqs_here, block_len, head_count, head_size)
    )
    row_delta = jnp.transpose(
        jnp.sum(grad_attn.astype(jnp.float32) * attn_vals, axis=-1), (0, 2, 1)
    )

    def back_block(grads_in, key_blk, value_blk, key_pos):

        def back_update(current):
            grad_query, grad_key, grad_value = current
            scores = (
                jnp.einsum("sqhd,skhd->shqk", queries, key_blk, preferred_element_type=jnp.float32)
                * score_scale
            )
            allowed = key_pos[:, None, None, :] <= positions[:, None, :, None]
            masked = jnp.where(allowed, scores, NEGATIVE)
            probability = jnp.exp(masked - log_total[..., None])
            prob_low = probability.astype(jnp.bfloat16)
            grad_value = grad_value + jnp.einsum(
                "shqk,sqhd->skhd", prob_low, grad_attn, preferred_element_type=jnp.float32
            )
            grad_prob = jnp.einsum(
                "sqhd,skhd->shqk", grad_attn, value_blk, preferred_element_type=jnp.float32
            )
            grad_score = (probability * (grad_prob - row_delta[..., None])).astype(jnp.bfloat16)
            grad_query = (
                grad_query
                + jnp.einsum(
                    "shqk,skhd->sqhd", grad_score, key_blk, preferred_element_type=jnp.float32
                )
                * score_scale
            )
            grad_key = (
                grad_key
                + jnp.einsum(
                    "shqk,sqhd->skhd", grad_score, queries, preferred_element_type=jnp.float32
                )
                * score_scale
            )
            return (grad_query, grad_key, grad_value)

        return lax.cond(
            jnp.min(key_pos) <= top_query, back_update, lambda unchanged: unchanged, grads_in
        )

    zero_rows = jnp.zeros((seqs_here, block_len, head_count, head_size), jnp.float32)

    def pass_back(grad_key, grad_value):
        return (
            shifted(grad_key.astype(jnp.bfloat16), "ctx", 1).astype(grad_key.dtype),
            shifted(grad_value.astype(jnp.bfloat16), "ctx", 1).astype(grad_value.dtype),
        )

    grad_query, grad_key, grad_value = back_block(
        (zero_rows, zero_rows, zero_rows), key_rows, value_rows, positions
    )
    grad_key, grad_value = pass_back(grad_key, grad_value)

    def cycle_backward(turn_index, carried):
        grad_query, key_cur, value_cur, grad_key, grad_value = carried
        key_cur, value_cur = shifted((key_cur, value_cur), "ctx", 1)
        source = (my_index - turn_index) % cycle_size
        key_pos = lax.dynamic_slice_in_dim(all_positions, source * block_len, block_len, 1)
        grad_query, grad_key, grad_value = back_block(
            (grad_query, grad_key, grad_value), key_cur, value_cur, key_pos
        )
        grad_key, grad_value = pass_back(grad_key, grad_value)
        return (grad_query, key_cur, value_cur, grad_key, grad_value)

    grad_query, unused_key, unused_value, grad_key, grad_value = lax.fori_loop(
        1, cycle_size, cycle_backward, (grad_query, key_rows, value_rows, grad_key, grad_value)
    )
    unused_rot, rotate_back = jax.vjp(
        lambda field_in: rotate(field_in, cosine, sine_table), zero_rows
    )
    query_pre = rotate_back(grad_query)[0]
    key_pre = rotate_back(grad_key)[0]
    grad_proj = (
        jnp.stack([query_pre, key_pre, grad_value], axis=2)
        .reshape(row_count, 3 * feature_count)
        .astype(jnp.bfloat16)
    )
    grad_qkv_bias = jnp.sum(grad_proj.astype(jnp.float32), axis=0)
    grad_qkv = jnp.einsum("rd,re->de", normed_one, grad_proj, preferred_element_type=jnp.float32)
    grad_one = jnp.einsum("re,de->rd", grad_proj, whole_qkv, preferred_element_type=jnp.float32)
    unused_one, norm_back_one = jax.vjp(layer_norm, inputs, ln1_gain, ln1_bias)
    input_one, grad_gain_one, grad_bias_one = norm_back_one(grad_one)
    unused_two, norm_back_two = jax.vjp(layer_norm, inputs, ln2_gain, ln2_bias)
    input_two, grad_gain_two, grad_bias_two = norm_back_two(grad_two)
    grad_input = (
        (cot_full + input_one + input_two)
        .astype(jnp.bfloat16)
        .reshape(seqs_here, block_len, feature_count)
    )
    summed = (
        lax.psum(grad_qkv.astype(jnp.bfloat16), "ctx").astype(jnp.float32),
        lax.psum(grad_out.astype(jnp.bfloat16), "ctx").astype(jnp.float32),
        lax.psum(grad_up.astype(jnp.bfloat16), "ctx").astype(jnp.float32),
        lax.psum(grad_down.astype(jnp.bfloat16), "ctx").astype(jnp.float32),
        lax.psum(grad_gain_one.astype(jnp.bfloat16), "ctx").astype(jnp.float32),
        lax.psum(grad_bias_one.astype(jnp.bfloat16), "ctx").astype(jnp.float32),
        lax.psum(grad_gain_two.astype(jnp.bfloat16), "ctx").astype(jnp.float32),
        lax.psum(grad_bias_two.astype(jnp.bfloat16), "ctx").astype(jnp.float32),
        lax.psum(grad_qkv_bias.astype(jnp.bfloat16), "ctx").astype(jnp.float32),
        lax.psum(grad_up_bias.astype(jnp.bfloat16), "ctx").astype(jnp.float32),
    )
    sum_qkv, sum_out, sum_up, sum_down = (
        lax.psum_scatter(
            summed[0].astype(jnp.bfloat16), "shard", scatter_dimension=0, tiled=True
        ).astype(jnp.float32),
        lax.psum_scatter(
            summed[1].astype(jnp.bfloat16), "shard", scatter_dimension=0, tiled=True
        ).astype(jnp.float32),
        lax.psum_scatter(
            summed[2].astype(jnp.bfloat16), "shard", scatter_dimension=0, tiled=True
        ).astype(jnp.float32),
        lax.psum_scatter(
            summed[3].astype(jnp.bfloat16), "shard", scatter_dimension=0, tiled=True
        ).astype(jnp.float32),
    )
    sum_small = (
        lax.psum(summed[4].astype(jnp.bfloat16), "shard").astype(jnp.float32),
        lax.psum(summed[5].astype(jnp.bfloat16), "shard").astype(jnp.float32),
        lax.psum(summed[6].astype(jnp.bfloat16), "shard").astype(jnp.float32),
        lax.psum(summed[7].astype(jnp.bfloat16), "shard").astype(jnp.float32),
        lax.psum(summed[8].astype(jnp.bfloat16), "shard").astype(jnp.float32),
        lax.psum(summed[9].astype(jnp.bfloat16), "shard").astype(jnp.float32),
    )
    return (
        layer_output,
        grad_input,
        sum_small[0],
        sum_small[1],
        sum_small[2],
        sum_small[3],
        sum_qkv,
        sum_small[4],
        sum_out,
        sum_up,
        sum_small[5],
        sum_down,
    )


def solution(mesh):
    placed = (
        P("shard", "ctx", None),
        P("shard", "ctx"),
        P("shard", "ctx", None),
        P(),
        P(),
        P(),
        P(),
        P("shard", None),
        P(),
        P("shard", None),
        P("shard", None),
        P(),
        P("shard", None),
    )
    return jax.shard_map(
        on_device,
        mesh=mesh,
        in_specs=placed,
        out_specs=(
            P("shard", "ctx", None),
            P("shard", "ctx", None),
            P(),
            P(),
            P(),
            P(),
            P("shard", None),
            P(),
            P("shard", None),
            P("shard", None),
            P(),
            P("shard", None),
        ),
        check_vma=False,
    )
```

profile of v0, /device:TPU:0, one launch (start us, length us, event | category | flops | bytes accessed | tf_op | source)
XLA Modules:
  0.0 602.1 jit_solution(3301122409901663954)
XLA Ops:
  12.0 14.1 %all_gather.16 = s32[1,1024]{1,0:T(1,128)} all-gather(s32[1,128]{1,0:T(1,128)S(1)} %copy-done.10), channel_id=1, replica_groups=mesh['shard'=4,'ctx'=8] {'ctx'}, dimensions={1}, use_global_device_ids=true | all-gather | bytes 4608 | tf_op jit(solution)/shard_map/all_gather | solution.py:78
  27.0 13.2 %all-gather.7.cloned.1.call-done = bf16[768,768]{1,0:T(8,128)(2,1)} async-done(((bf16[192,768]{1,0:T(8,128)(2,1)}), bf16[768,768]{1,0:T(8,128)(2,1)}) %all-gather.7.cloned.1.call-update) | async-done | bytes 1179664 | tf_op jit(solution)/shard_map/all_gather | solution.py:74
  42.1 47.0 %all-gather.5.cloned.1.call-done = bf16[768,2304]{1,0:T(8,128)(2,1)} async-done(((bf16[192,2304]{1,0:T(8,128)(2,1)}), bf16[768,2304]{1,0:T(8,128)(2,1)}) %all-gather.5.cloned.1.call-update) | async-done | bytes 3538960 | tf_op jit(solution)/shard_map/all_gather | solution.py:73
  94.8 72.4 %while.46 = (s32[]{:T(128)}, f32[1,12,128]{2,1,0:T(8,128)}, f32[1,12,128]{2,1,0:T(8,128)S(1)}, f32[1,128,12,64]{1,3,2,0:T(8,128)S(1)}, bf16[1,128,12,64]{1,3,2,0...) while((s32[]{:T(128)}, f32[1,12,128]{2,1,0:T(8,128)}, ...), condition=%wide.region_14.15_spmd, body=%wide.region_8.14_spmd.sunk | while | flops 52318864 | bytes 6261282 | solution.py:133
  130.6 4.2 collective-permute-done.1
  171.6 6.8 %collective-permute-done.7 = bf16[1,128,12,64]{1,3,2,0:T(8,128)(2,1)S(1)} collective-permute-done((bf16[1,128,12,64]{1,3,2,0:T(8,128)(2,1)S(1)}, bf16[1,128,12,64]{1,3,2,0:T(8,128)(2,1)S(1)}, u32[]{:S(2)}, u32[]{:S(2)}) %collective-permute-start.7) | collective-permute-done | bytes 196640 | tf_op jit(solution)/shard_map/ppermute | solution.py:15
  180.5 132.8 %while.47 = (s32[]{:T(128)}, f32[1,128,12,64]{1,3,2,0:T(8,128)S(1)}, bf16[1,128,12,64]{1,3,2,0:T(8,128)(2,1)S(1)}, bf16[1,128,12,64]{1,3,2,0:T(8,128)(2,1)S(1)},...) while((s32[]{:T(128)}, ...), condition=%wide.region_22.23_spmd, body=%wide.region_18.0_spmd.sunk | while | flops 128106640 | bytes 13613730 | solution.py:230
  183.2 4.3 collective-permute-done.3
  191.7 6.7 %collective-permute-done.5 = bf16[1,128,12,64]{1,3,2,0:T(8,128)(2,1)S(1)} collective-permute-done((bf16[1,128,12,64]{1,3,2,0:T(8,128)(2,1)S(1)}, bf16[1,128,12,64]{1,3,2,0:T(8,128)(2,1)S(1)}, u32[]{:S(2)}, u32[]{:S(2)}) %collective-permute-start.5) | collective-permute-done | bytes 196640 | tf_op jit(solution)/shard_map/while/body/eval_jaxpr/ppermute | solution.py:15
  211.7 6.7 %collective-permute-done.5 = bf16[1,128,12,64]{1,3,2,0:T(8,128)(2,1)S(1)} collective-permute-done((bf16[1,128,12,64]{1,3,2,0:T(8,128)(2,1)S(1)}, bf16[1,128,12,64]{1,3,2,0:T(8,128)(2,1)S(1)}, u32[]{:S(2)}, u32[]{:S(2)}) %collective-permute-start.5) | collective-permute-done | bytes 196640 | tf_op jit(solution)/shard_map/while/body/eval_jaxpr/ppermute | solution.py:15
  229.9 6.7 %collective-permute-done.5 = bf16[1,128,12,64]{1,3,2,0:T(8,128)(2,1)S(1)} collective-permute-done((bf16[1,128,12,64]{1,3,2,0:T(8,128)(2,1)S(1)}, bf16[1,128,12,64]{1,3,2,0:T(8,128)(2,1)S(1)}, u32[]{:S(2)}, u32[]{:S(2)}) %collective-permute-start.5) | collective-permute-done | bytes 196640 | tf_op jit(solution)/shard_map/while/body/eval_jaxpr/ppermute | solution.py:15
  248.1 6.7 %collective-permute-done.5 = bf16[1,128,12,64]{1,3,2,0:T(8,128)(2,1)S(1)} collective-permute-done((bf16[1,128,12,64]{1,3,2,0:T(8,128)(2,1)S(1)}, bf16[1,128,12,64]{1,3,2,0:T(8,128)(2,1)S(1)}, u32[]{:S(2)}, u32[]{:S(2)}) %collective-permute-start.5) | collective-permute-done | bytes 196640 | tf_op jit(solution)/shard_map/while/body/eval_jaxpr/ppermute | solution.py:15
  266.3 6.7 %collective-permute-done.5 = bf16[1,128,12,64]{1,3,2,0:T(8,128)(2,1)S(1)} collective-permute-done((bf16[1,128,12,64]{1,3,2,0:T(8,128)(2,1)S(1)}, bf16[1,128,12,64]{1,3,2,0:T(8,128)(2,1)S(1)}, u32[]{:S(2)}, u32[]{:S(2)}) %collective-permute-start.5) | collective-permute-done | bytes 196640 | tf_op jit(solution)/shard_map/while/body/eval_jaxpr/ppermute | solution.py:15
  286.3 6.7 %collective-permute-done.5 = bf16[1,128,12,64]{1,3,2,0:T(8,128)(2,1)S(1)} collective-permute-done((bf16[1,128,12,64]{1,3,2,0:T(8,128)(2,1)S(1)}, bf16[1,128,12,64]{1,3,2,0:T(8,128)(2,1)S(1)}, u32[]{:S(2)}, u32[]{:S(2)}) %collective-permute-start.5) | collective-permute-done | bytes 196640 | tf_op jit(solution)/shard_map/while/body/eval_jaxpr/ppermute | solution.py:15
  304.5 6.7 %collective-permute-done.5 = bf16[1,128,12,64]{1,3,2,0:T(8,128)(2,1)S(1)} collective-permute-done((bf16[1,128,12,64]{1,3,2,0:T(8,128)(2,1)S(1)}, bf16[1,128,12,64]{1,3,2,0:T(8,128)(2,1)S(1)}, u32[]{:S(2)}, u32[]{:S(2)}) %collective-permute-start.5) | collective-permute-done | bytes 196640 | tf_op jit(solution)/shard_map/while/body/eval_jaxpr/ppermute | solution.py:15
  317.9 8.4 %multiply_convert_fusion = (bf16[128,3072]{1,0:T(8,128)(2,1)S(1)}, f32[128,3072]{1,0:T(8,128)}, f32[128,3072]{1,0:T(8,128)}) fusion(f32[3072]{0:T(1024)S(1)} %copy-done.22, bf16[768,3072]{1,0:T(8,128)(2,1)} %all-gather.9.cloned.1.call-done, bf16[1,128,768]{2,1,0:T(8,128)(2,1)S(1)} %copy-done, f32[768]{0:T(1024)S(1)} %copy-done.12, f32[768]{0:T(1024)S(1)} %copy-done.9, ...), kind=kOutput, calls=%fused_computation.94 | convolution fusion | flops 630521856 | bytes 8866816 | tf_op jit(solution)/shard_map/dot_general | solution.py:140
  326.3 5.0 fusion.129
  338.8 4.7 fusion.131
  345.1 35.6 %reduce-scatter.5.cloned.1.call-done = bf16[192,2304]{1,0:T(8,128)(2,1)} async-done(((bf16[768,2304]{1,0:T(8,128)(2,1)}), bf16[192,2304]{1,0:T(8,128)(2,1)}) %reduce-scatter.5.cloned.1.call-update) | async-done | bytes 884752 | tf_op jit(solution)/shard_map/reduce_scatter | solution.py:268
  380.7 60.0 %reduce-scatter.9.cloned.1.call-done = bf16[192,3072]{1,0:T(8,128)(2,1)} async-done(((bf16[768,3072]{1,0:T(8,128)(2,1)}), bf16[192,3072]{1,0:T(8,128)(2,1)}) %reduce-scatter.9.cloned.1.call-update) | async-done | bytes 1179664 | tf_op jit(solution)/shard_map/reduce_scatter | solution.py:274
  440.7 60.0 %reduce-scatter.11.cloned.1.call-done = bf16[768,768]{1,0:T(8,128)(2,1)} async-done(((bf16[3072,768]{1,0:T(8,128)(2,1)}), bf16[768,768]{1,0:T(8,128)(2,1)}) %reduce-scatter.11.cloned.1.call-update) | async-done | bytes 1179664 | tf_op jit(solution)/shard_map/reduce_scatter | solution.py:277
  501.8 29.7 %all-reduce.6 = (bf16[768]{0:T(1024)(128)(2,1)S(1)}, bf16[768]{0:T(1024)(128)(2,1)S(1)}, bf16[768]{0:T(1024)(128)(2,1)S(1)}, bf16[768]{0:T(1024)(128)(2,1)S(1)},...) all-reduce(bf16[768]{0:T(1024)(128)(2,1)S(1)} %get-tuple-element.78, ...), channel_id=1, replica_groups=mesh['shard'=4,'ctx'=8] {'ctx'}, use_global_device_ids=true, to_apply=%region_28.29 | all-reduce | flops 8448 | bytes 33792 | tf_op jit(solution)/shard_map/psum | solution.py:260
  531.4 15.3 %all-reduce.8 = (bf16[768]{0:T(1024)(128)(2,1)S(1)}, bf16[768]{0:T(1024)(128)(2,1)S(1)}, bf16[768]{0:T(1024)(128)(2,1)S(1)}, bf16[768]{0:T(1024)(128)(2,1)S(1)},...) all-reduce(bf16[768]{0:T(1024)(128)(2,1)S(1)} %get-tuple-element.84, ...), channel_id=1, replica_groups=mesh['shard'=4,'ctx'=8] {'shard'}, use_global_device_ids=true, to_apply=%region_29.30 | all-reduce | flops 8448 | bytes 33792 | tf_op jit(solution)/shard_map/psum | solution.py:282
  555.7 32.2 %all-reduce.11.cloned.1.call-done = (bf16[192,2304]{1,0:T(8,128)(2,1)}, bf16[192,768]{1,0:T(8,128)(2,1)}, bf16[192,3072]{1,0:T(8,128)(2,1)}, bf16[768,768]{1,0:T(8,128)(2,1)}) async-done(((bf16[192,2304]{1,0:T(8,128)(2,1)}, bf16[192,768]{1,0:T(8,128)(2,1)}, bf16[192,3072]{1,0:T(8,128)(2,1)}, bf16[768,768]{1,0:T(8,128)(2,1)}), (bf16[192,2304]{1,0:T(8,128)(2,1)}, bf16[192,768]{1,0:T(8,128)(2,1)}, ...) | async-done | bytes 3538960 | tf_op jit(solution)/shard_map/psum | solution.py:256
  (338 shorter events, 197.3 us)
Async XLA Ops:
  7.2 33.0 %all-gather.7.cloned.1.call-start = ((), (), s32[]{:S(2)}) async-start(), calls=%async_computation.5 | async-start | bytes 1474560 | tf_op jit(solution)/shard_map/all_gather | solution.py:74
  7.9 81.2 %all-gather.5.cloned.1.call-start = ((), (), s32[]{:S(2)}) async-start(), calls=%async_computation.4 | async-start | bytes 4423680 | tf_op jit(solution)/shard_map/all_gather | solution.py:73
  8.7 308.8 %all-gather.9.cloned.1.call-start = ((), (), s32[]{:S(2)}) async-start(), calls=%async_computation.6 | async-start | bytes 5898240 | tf_op jit(solution)/shard_map/all_gather | solution.py:75
  9.5 316.8 %all-gather.11.cloned.1.call-start = ((), (), s32[]{:S(2)}) async-start(), calls=%async_computation.7 | async-start | bytes 5898240 | tf_op jit(solution)/shard_map/all_gather | solution.py:76
  10.0 335.0 %reduce-scatter.7.cloned.1.call-start = ((), (), s32[]{:S(2)}) async-start(), calls=%async_computation.9 | async-start | bytes 1474560 | tf_op jit(solution)/shard_map/reduce_scatter | solution.py:271
  94.8 9.0 %collective-permute-start = (bf16[1,128,12,64]{1,3,2,0:T(8,128)(2,1)S(1)}, bf16[1,128,12,64]{1,3,2,0:T(8,128)(2,1)S(1)}, u32[]{:S(2)}, u32[]{:S(2)}) collective-permute-start(bf16[1,128,12,64]{1,3,2,0:T(8,128)(2,1)S(1)} %get-tuple-element.1113), channel_id=1, source_target_pairs={{0,1},{1,2},{2,3},{3,4},{4,5},{5,6},{6,7},{7,0},{8,9},{9,10},{10,1... | collective-permute-start | bytes 589832 | tf_op jit(solution)/shard_map/while/body/eval_jaxpr/ppermute | solution.py:15
  106.8 9.0 %collective-permute-start = (bf16[1,128,12,64]{1,3,2,0:T(8,128)(2,1)S(1)}, bf16[1,128,12,64]{1,3,2,0:T(8,128)(2,1)S(1)}, u32[]{:S(2)}, u32[]{:S(2)}) collective-permute-start(bf16[1,128,12,64]{1,3,2,0:T(8,128)(2,1)S(1)} %get-tuple-element.1113), channel_id=1, source_target_pairs={{0,1},{1,2},{2,3},{3,4},{4,5},{5,6},{6,7},{7,0},{8,9},{9,10},{10,1... | collective-permute-start | bytes 589832 | tf_op jit(solution)/shard_map/while/body/eval_jaxpr/ppermute | solution.py:15
  118.8 9.0 %collective-permute-start = (bf16[1,128,12,64]{1,3,2,0:T(8,128)(2,1)S(1)}, bf16[1,128,12,64]{1,3,2,0:T(8,128)(2,1)S(1)}, u32[]{:S(2)}, u32[]{:S(2)}) collective-permute-start(bf16[1,128,12,64]{1,3,2,0:T(8,128)(2,1)S(1)} %get-tuple-element.1113), channel_id=1, source_target_pairs={{0,1},{1,2},{2,3},{3,4},{4,5},{5,6},{6,7},{7,0},{8,9},{9,10},{10,1... | collective-permute-start | bytes 589832 | tf_op jit(solution)/shard_map/while/body/eval_jaxpr/ppermute | solution.py:15
  127.9 9.0 %collective-permute-start = (bf16[1,128,12,64]{1,3,2,0:T(8,128)(2,1)S(1)}, bf16[1,128,12,64]{1,3,2,0:T(8,128)(2,1)S(1)}, u32[]{:S(2)}, u32[]{:S(2)}) collective-permute-start(bf16[1,128,12,64]{1,3,2,0:T(8,128)(2,1)S(1)} %get-tuple-element.1113), channel_id=1, source_target_pairs={{0,1},{1,2},{2,3},{3,4},{4,5},{5,6},{6,7},{7,0},{8,9},{9,10},{10,1... | collective-permute-start | bytes 589832 | tf_op jit(solution)/shard_map/while/body/eval_jaxpr/ppermute | solution.py:15
  137.0 9.0 %collective-permute-start = (bf16[1,128,12,64]{1,3,2,0:T(8,128)(2,1)S(1)}, bf16[1,128,12,64]{1,3,2,0:T(8,128)(2,1)S(1)}, u32[]{:S(2)}, u32[]{:S(2)}) collective-permute-start(bf16[1,128,12,64]{1,3,2,0:T(8,128)(2,1)S(1)} %get-tuple-element.1113), channel_id=1, source_target_pairs={{0,1},{1,2},{2,3},{3,4},{4,5},{5,6},{6,7},{7,0},{8,9},{9,10},{10,1... | collective-permute-start | bytes 589832 | tf_op jit(solution)/shard_map/while/body/eval_jaxpr/ppermute | solution.py:15
  146.2 9.0 %collective-permute-start = (bf16[1,128,12,64]{1,3,2,0:T(8,128)(2,1)S(1)}, bf16[1,128,12,64]{1,3,2,0:T(8,128)(2,1)S(1)}, u32[]{:S(2)}, u32[]{:S(2)}) collective-permute-start(bf16[1,128,12,64]{1,3,2,0:T(8,128)(2,1)S(1)} %get-tuple-element.1113), channel_id=1, source_target_pairs={{0,1},{1,2},{2,3},{3,4},{4,5},{5,6},{6,7},{7,0},{8,9},{9,10},{10,1... | collective-permute-start | bytes 589832 | tf_op jit(solution)/shard_map/while/body/eval_jaxpr/ppermute | solution.py:15
  158.2 9.0 %collective-permute-start = (bf16[1,128,12,64]{1,3,2,0:T(8,128)(2,1)S(1)}, bf16[1,128,12,64]{1,3,2,0:T(8,128)(2,1)S(1)}, u32[]{:S(2)}, u32[]{:S(2)}) collective-permute-start(bf16[1,128,12,64]{1,3,2,0:T(8,128)(2,1)S(1)} %get-tuple-element.1113), channel_id=1, source_target_pairs={{0,1},{1,2},{2,3},{3,4},{4,5},{5,6},{6,7},{7,0},{8,9},{9,10},{10,1... | collective-permute-start | bytes 589832 | tf_op jit(solution)/shard_map/while/body/eval_jaxpr/ppermute | solution.py:15
  168.8 211.9 %reduce-scatter.5.cloned.1.call-start = ((), (), s32[]{:S(2)}) async-start(), calls=%async_computation.8 | async-start | bytes 4423680 | tf_op jit(solution)/shard_map/reduce_scatter | solution.py:268
  171.5 8.9 %collective-permute-start.6 = (bf16[1,128,12,64]{1,3,2,0:T(8,128)(2,1)S(1)}, bf16[1,128,12,64]{1,3,2,0:T(8,128)(2,1)S(1)}, u32[]{:S(2)}, u32[]{:S(2)}) collective-permute-start(bf16[1,128,12,64]{1,3,2,0:T(8,128)(2,1)S(1)} %convert_element_type.289), channel_id=1, source_target_pairs={{0,1},{1,2},{2,3},{3,4},{4,5},{5,6},{6,7},{7,0},{8,9},{9,10},{10,1... | collective-permute-start | bytes 589832 | tf_op jit(solution)/shard_map/ppermute | solution.py:15
  180.6 9.0 %collective-permute-start.2 = (bf16[1,128,12,64]{1,3,2,0:T(8,128)(2,1)S(1)}, bf16[1,128,12,64]{1,3,2,0:T(8,128)(2,1)S(1)}, u32[]{:S(2)}, u32[]{:S(2)}) collective-permute-start(bf16[1,128,12,64]{1,3,2,0:T(8,128)(2,1)S(1)} %get-tuple-element.1171), channel_id=1, source_target_pairs={{0,1},{1,2},{2,3},{3,4},{4,5},{5,6},{6,7},{7,0},{8,9},{9,10},{10,1... | collective-permute-start | bytes 589832 | tf_op jit(solution)/shard_map/while/body/eval_jaxpr/ppermute | solution.py:15
  200.6 9.0 %collective-permute-start.2 = (bf16[1,128,12,64]{1,3,2,0:T(8,128)(2,1)S(1)}, bf16[1,128,12,64]{1,3,2,0:T(8,128)(2,1)S(1)}, u32[]{:S(2)}, u32[]{:S(2)}) collective-permute-start(bf16[1,128,12,64]{1,3,2,0:T(8,128)(2,1)S(1)} %get-tuple-element.1171), channel_id=1, source_target_pairs={{0,1},{1,2},{2,3},{3,4},{4,5},{5,6},{6,7},{7,0},{8,9},{9,10},{10,1... | collective-permute-start | bytes 589832 | tf_op jit(solution)/shard_map/while/body/eval_jaxpr/ppermute | solution.py:15
  220.7 9.0 %collective-permute-start.2 = (bf16[1,128,12,64]{1,3,2,0:T(8,128)(2,1)S(1)}, bf16[1,128,12,64]{1,3,2,0:T(8,128)(2,1)S(1)}, u32[]{:S(2)}, u32[]{:S(2)}) collective-permute-start(bf16[1,128,12,64]{1,3,2,0:T(8,128)(2,1)S(1)} %get-tuple-element.1171), channel_id=1, source_target_pairs={{0,1},{1,2},{2,3},{3,4},{4,5},{5,6},{6,7},{7,0},{8,9},{9,10},{10,1... | collective-permute-start | bytes 589832 | tf_op jit(solution)/shard_map/while/body/eval_jaxpr/ppermute | solution.py:15
  238.8 9.0 %collective-permute-start.2 = (bf16[1,128,12,64]{1,3,2,0:T(8,128)(2,1)S(1)}, bf16[1,128,12,64]{1,3,2,0:T(8,128)(2,1)S(1)}, u32[]{:S(2)}, u32[]{:S(2)}) collective-permute-start(bf16[1,128,12,64]{1,3,2,0:T(8,128)(2,1)S(1)} %get-tuple-element.1171), channel_id=1, source_target_pairs={{0,1},{1,2},{2,3},{3,4},{4,5},{5,6},{6,7},{7,0},{8,9},{9,10},{10,1... | collective-permute-start | bytes 589832 | tf_op jit(solution)/shard_map/while/body/eval_jaxpr/ppermute | solution.py:15
  257.0 9.0 %collective-permute-start.2 = (bf16[1,128,12,64]{1,3,2,0:T(8,128)(2,1)S(1)}, bf16[1,128,12,64]{1,3,2,0:T(8,128)(2,1)S(1)}, u32[]{:S(2)}, u32[]{:S(2)}) collective-permute-start(bf16[1,128,12,64]{1,3,2,0:T(8,128)(2,1)S(1)} %get-tuple-element.1171), channel_id=1, source_target_pairs={{0,1},{1,2},{2,3},{3,4},{4,5},{5,6},{6,7},{7,0},{8,9},{9,10},{10,1... | collective-permute-start | bytes 589832 | tf_op jit(solution)/shard_map/while/body/eval_jaxpr/ppermute | solution.py:15
  275.2 9.0 %collective-permute-start.2 = (bf16[1,128,12,64]{1,3,2,0:T(8,128)(2,1)S(1)}, bf16[1,128,12,64]{1,3,2,0:T(8,128)(2,1)S(1)}, u32[]{:S(2)}, u32[]{:S(2)}) collective-permute-start(bf16[1,128,12,64]{1,3,2,0:T(8,128)(2,1)S(1)} %get-tuple-element.1171), channel_id=1, source_target_pairs={{0,1},{1,2},{2,3},{3,4},{4,5},{5,6},{6,7},{7,0},{8,9},{9,10},{10,1... | collective-permute-start | bytes 589832 | tf_op jit(solution)/shard_map/while/body/eval_jaxpr/ppermute | solution.py:15
  295.3 9.0 %collective-permute-start.2 = (bf16[1,128,12,64]{1,3,2,0:T(8,128)(2,1)S(1)}, bf16[1,128,12,64]{1,3,2,0:T(8,128)(2,1)S(1)}, u32[]{:S(2)}, u32[]{:S(2)}) collective-permute-start(bf16[1,128,12,64]{1,3,2,0:T(8,128)(2,1)S(1)} %get-tuple-element.1171), channel_id=1, source_target_pairs={{0,1},{1,2},{2,3},{3,4},{4,5},{5,6},{6,7},{7,0},{8,9},{9,10},{10,1... | collective-permute-start | bytes 589832 | tf_op jit(solution)/shard_map/while/body/eval_jaxpr/ppermute | solution.py:15
  317.2 123.5 %reduce-scatter.9.cloned.1.call-start = ((), (), s32[]{:S(2)}) async-start(), calls=%async_computation.10 | async-start | bytes 5898240 | tf_op jit(solution)/shard_map/reduce_scatter | solution.py:274
  335.1 165.6 %reduce-scatter.11.cloned.1.call-start = ((), (), s32[]{:S(2)}) async-start(), calls=%async_computation.11 | async-start | bytes 5898240 | tf_op jit(solution)/shard_map/reduce_scatter | solution.py:277
  338.7 249.2 %all-reduce.11.cloned.1.call-start = ((), (), s32[]{:S(2)}) async-start(), calls=%async_computation.12 | async-start | bytes 7077888 | tf_op jit(solution)/shard_map/psum | solution.py:256
  (52 other events, 815.8 us)
Sparse Core Ops, SparseCore 0:
  9.8 30.2 all-gather.6
  42.0 47.1 all-gather.4
  91.0 56.9 all-gather.8
  149.7 56.9 all-gather.10
  210.0 28.7 reduce-scatter.6
  317.3 63.3 reduce-scatter.4
  383.7 56.9 reduce-scatter.8
  443.7 56.9 reduce-scatter.10
  503.3 84.5 all-reduce.10
where the time goes:
time: 604 us; the launch traced here: 602 us
  waiting for transfers between devices  408 us (68%)
  blocking collectives  59 us (10%)
  matrix products  49.6 us (8%)
  other arithmetic  40.6 us (7%)
  loops' own time  19.8 us (3%)
  between operations  15.6 us (3%)
    ppermute x44, waiting for transfers between devices, shifted(): lax.ppermute(shard, axis, [(i, (i + by) % count) for i in range(count)])  157 us
    reduce_scatter x1, waiting for transfers between devices, on_device(): lax.psum_scatter(summed[2].astype(jnp.bfloat16), 'shard', scatter_dimensi...  60 us
    reduce_scatter x1, waiting for transfers between devices, on_device(): lax.psum_scatter(summed[3].astype(jnp.bfloat16), 'shard', scatter_dimensi...  60 us
    all_gather x1, waiting for transfers between devices, on_device(): lax.all_gather(w_qkv, 'shard', axis=0, tiled=True)  47 us
    reduce_scatter x1, waiting for transfers between devices, on_device(): lax.psum_scatter(summed[0].astype(jnp.bfloat16), 'shard', scatter_dimensi...  35.6 us
    psum x1, waiting for transfers between devices, on_device(): lax.psum(grad_qkv.astype(jnp.bfloat16), 'ctx').astype(jnp.float32)  32.2 us
    psum x1, blocking collectives, on_device(): lax.psum(grad_gain_one.astype(jnp.bfloat16), 'ctx').astype(jnp.float32)  29.7 us
    psum x1, blocking collectives, on_device(): lax.psum(summed[4].astype(jnp.bfloat16), 'shard').astype(jnp.float32)  15.3 us
  transfers between devices with their start and end apart: 53, of which 50 were waited for; matrix products, arithmetic and copies ran while one was open for 14% of the time, Pallas kernels for 0%

commit v1 on v0

--- a/solution.py
+++ b/solution.py
@@ -253,7 +253,7 @@
         .reshape(seqs_here, block_len, feature_count)
     )
     summed = (
-        lax.psum(grad_qkv.astype(jnp.bfloat16), "ctx").astype(jnp.float32),
+        jnp.sum(lax.all_gather(grad_qkv.astype(jnp.bfloat16), "ctx"), axis=0).astype(jnp.float32),
         lax.psum(grad_out.astype(jnp.bfloat16), "ctx").astype(jnp.float32),
         lax.psum(grad_up.astype(jnp.bfloat16), "ctx").astype(jnp.float32),
         lax.psum(grad_down.astype(jnp.bfloat16), "ctx").astype(jnp.float32),

time: 604 us -> 763 us (1.26)
  waiting for transfers between devices: 408 us -> 542 us
  other arithmetic: 40.6 us -> 58.6 us
    all_gather x0 -> x1, waiting for transfers between devices: none -> 255 us  [on_device(): lax.all_gather(grad_qkv.astype(jnp.bfloat16), 'ctx')]
    reduce_scatter x1, waiting for transfers between devices: 60 us -> 0.02 us  [on_device(): lax.psum_scatter(summed[2].astype(jnp.bfloat16), 'shard', scatter_dimensi...]
    reduce_scatter x1, waiting for transfers between devices: 60 us -> 0.02 us  [on_device(): lax.psum_scatter(summed[3].astype(jnp.bfloat16), 'shard', scatter_dimensi...]
    psum x1, waiting for transfers between devices: 32.2 us -> 0.01 us  [on_device(): lax.psum(grad_out.astype(jnp.bfloat16), 'ctx').astype(jnp.float32)]
    all_gather x1, waiting for transfers between devices: 0.01 us -> 25.6 us  [on_device(): lax.all_gather(w_down, 'shard', axis=0, tiled=True)]
    reduce_sum x0 -> x1, other arithmetic: none -> 12.8 us  [on_device(): jnp.sum(lax.all_gather(grad_qkv.astype(jnp.bfloat16), 'ctx'), axis=0)]
  transfers between devices with their start and end apart: 53 -> 54, of which waited for: 50 -> 49; matrix products, arithmetic and copies ran while one was open for 14% -> 15% of each run, Pallas kernels for 0% -> 0%
where the time goes in v1:
time: 763 us; the launch traced here: 761 us
  waiting for transfers between devices  542 us (71%)
  other arithmetic  58.6 us (8%)
  blocking collectives  56.5 us (7%)
  matrix products  52.4 us (7%)
  loops' own time  19.8 us (3%)
  between operations  16 us (2%)
  local copies, waits for them, and re-layouts  9.28 us (1%)
    all_gather x1, waiting for transfers between devices, on_device(): lax.all_gather(grad_qkv.astype(jnp.bfloat16), 'ctx')  255 us
    ppermute x44, waiting for transfers between devices, shifted(): lax.ppermute(shard, axis, [(i, (i + by) % count) for i in range(count)])  156 us
    all_gather x1, waiting for transfers between devices, on_device(): lax.all_gather(w_qkv, 'shard', axis=0, tiled=True)  47 us
    reduce_scatter x1, waiting for transfers between devices, on_device(): lax.psum_scatter(summed[0].astype(jnp.bfloat16), 'shard', scatter_dimensi...  41.2 us
    psum x1, blocking collectives, on_device(): lax.psum(grad_gain_one.astype(jnp.bfloat16), 'ctx').astype(jnp.float32)  26.7 us
    all_gather x1, waiting for transfers between devices, on_device(): lax.all_gather(w_down, 'shard', axis=0, tiled=True)  25.6 us
    psum x1, blocking collectives, on_device(): lax.psum(summed[4].astype(jnp.bfloat16), 'shard').astype(jnp.float32)  16.3 us
  transfers between devices with their start and end apart: 54, of which 49 were waited for; matrix products, arithmetic and copies ran while one was open for 15% of the time, Pallas kernels for 0%

profile of v1, /device:TPU:0, one launch (start us, length us, event | category | flops | bytes accessed | tf_op | source)
XLA Modules:
  0.0 760.9 jit_solution(6784640421905243372)
XLA Ops:
  12.0 13.5 %all_gather.22 = s32[1,1024]{1,0:T(1,128)S(1)} all-gather(s32[1,128]{1,0:T(1,128)S(1)} %copy-done.10), channel_id=1, replica_groups=mesh['shard'=4,'ctx'=8] {'ctx'}, dimensions={1}, use_global_device_ids=true | all-gather | bytes 4608 | tf_op jit(solution)/shard_map/all_gather | solution.py:78
  26.5 13.7 %all-gather.9.cloned.1.call-done = bf16[768,768]{1,0:T(8,128)(2,1)} async-done(((bf16[192,768]{1,0:T(8,128)(2,1)}), bf16[768,768]{1,0:T(8,128)(2,1)}) %all-gather.9.cloned.1.call-update) | async-done | bytes 1179664 | tf_op jit(solution)/shard_map/all_gather | solution.py:74
  42.1 47.0 %all-gather.7.cloned.1.call-done = bf16[768,2304]{1,0:T(8,128)(2,1)} async-done(((bf16[192,2304]{1,0:T(8,128)(2,1)}), bf16[768,2304]{1,0:T(8,128)(2,1)}) %all-gather.7.cloned.1.call-update) | async-done | bytes 3538960 | tf_op jit(solution)/shard_map/all_gather | solution.py:73
  97.9 72.5 %while.46 = (s32[]{:T(128)}, f32[1,12,128]{2,1,0:T(8,128)}, f32[1,12,128]{2,1,0:T(8,128)S(1)}, f32[1,128,12,64]{1,3,2,0:T(8,128)S(1)}, bf16[1,128,12,64]{1,3,2,0...) while((s32[]{:T(128)}, f32[1,12,128]{2,1,0:T(8,128)}, ...), condition=%wide.region_14.15_spmd, body=%wide.region_8.14_spmd.sunk | while | flops 52318864 | bytes 6261282 | solution.py:133
  112.0 4.9 collective-permute-done
  124.0 4.9 collective-permute-done
  133.1 4.9 collective-permute-done
  172.7 8.4 %multiply_convert_fusion = (bf16[128,3072]{1,0:T(8,128)(2,1)S(1)}, f32[128,3072]{1,0:T(8,128)}, f32[128,3072]{1,0:T(8,128)}) fusion(f32[3072]{0:T(1024)S(1)} %copy-done.27, bf16[768,3072]{1,0:T(8,128)(2,1)} %all-gather.11.cloned.1.call-done, bf16[1,128,768]{2,1,0:T(8,128)(2,1)S(1)} %copy-done, f32[768]{0:T(1024)S(1)} %copy-done.13, f32[768]{0:T(1024)S(1)} %copy-done.9, ...), kind=kOutput, calls=%fused_computation.94 | convolution fusion | flops 630521856 | bytes 8866816 | tf_op jit(solution)/shard_map/dot_general | solution.py:140
  181.1 25.6 %all-gather.13.cloned.1.call-done = bf16[3072,768]{1,0:T(8,128)(2,1)} async-done(((bf16[768,768]{1,0:T(8,128)(2,1)}), bf16[3072,768]{1,0:T(8,128)(2,1)}) %all-gather.13.cloned.1.call-update) | async-done | bytes 4718608 | tf_op jit(solution)/shard_map/all_gather | solution.py:76
  206.7 5.6 fusion.129
  226.3 5.2 collective-permute-done.6
  234.6 137.0 %while.47 = (s32[]{:T(128)}, f32[1,128,12,64]{1,3,2,0:T(8,128)S(1)}, bf16[1,128,12,64]{1,3,2,0:T(8,128)(2,1)S(1)}, bf16[1,128,12,64]{1,3,2,0:T(8,128)(2,1)S(1)},...) while((s32[]{:T(128)}, ...), condition=%wide.region_22.23_spmd, body=%wide.region_18.0_spmd.sunk | while | flops 128106640 | bytes 13613730 | solution.py:230
  247.2 6.7 collective-permute-done.4
  268.6 6.7 collective-permute-done.4
  286.8 6.7 collective-permute-done.4
  305.0 6.7 collective-permute-done.4
  323.1 6.7 collective-permute-done.4
  344.6 6.7 collective-permute-done.4
  362.7 6.7 collective-permute-done.4
  376.8 255.1 %all-gather.15.cloned.1.call-done = bf16[6144,2304]{1,0:T(8,128)(2,1)} async-done(((bf16[768,2304]{1,0:T(8,128)(2,1)}), bf16[6144,2304]{1,0:T(8,128)(2,1)}) %all-gather.15.cloned.1.call-update) | async-done | bytes 28311568 | tf_op jit(solution)/shard_map/all_gather | solution.py:256
  632.0 12.8 %reduce_sum.192 = bf16[768,2304]{1,0:T(8,128)(2,1)} reduce(bf16[8,768,2304]{2,1,0:T(8,128)(2,1)} %bitcast.279, bf16[]{:T(256)} %constant.272.clone.1), dimensions={0}, to_apply=%region_39.40 | reduce | flops 12386304 | bytes 31850498 | tf_op jit(solution)/shard_map/reduce_sum | solution.py:256
  652.0 26.7 %all-reduce.6 = (bf16[768]{0:T(1024)(128)(2,1)S(1)}, bf16[768]{0:T(1024)(128)(2,1)S(1)}, bf16[768]{0:T(1024)(128)(2,1)S(1)}, bf16[768]{0:T(1024)(128)(2,1)S(1)},...) all-reduce(bf16[768]{0:T(1024)(128)(2,1)S(1)} %get-tuple-element.78, ...), channel_id=1, replica_groups=mesh['shard'=4,'ctx'=8] {'ctx'}, use_global_device_ids=true, to_apply=%region_28.29 | all-reduce | flops 8448 | bytes 33792 | tf_op jit(solution)/shard_map/psum | solution.py:260
  678.7 16.3 %all-reduce.8 = (bf16[768]{0:T(1024)(128)(2,1)S(1)}, bf16[768]{0:T(1024)(128)(2,1)S(1)}, bf16[768]{0:T(1024)(128)(2,1)S(1)}, bf16[768]{0:T(1024)(128)(2,1)S(1)},...) all-reduce(bf16[768]{0:T(1024)(128)(2,1)S(1)} %get-tuple-element.84, ...), channel_id=1, replica_groups=mesh['shard'=4,'ctx'=8] {'shard'}, use_global_device_ids=true, to_apply=%region_29.30 | all-reduce | flops 8448 | bytes 33792 | tf_op jit(solution)/shard_map/psum | solution.py:282
  710.4 41.2 %reduce-scatter.5.cloned.1.call-done = bf16[192,2304]{1,0:T(8,128)(2,1)} async-done(((bf16[768,2304]{1,0:T(8,128)(2,1)}), bf16[192,2304]{1,0:T(8,128)(2,1)}) %reduce-scatter.5.cloned.1.call-update) | async-done | bytes 884752 | tf_op jit(solution)/shard_map/reduce_scatter | solution.py:268
  (352 shorter events, 215.3 us)
Async XLA Ops:
  7.2 33.0 %all-gather.9.cloned.1.call-start = ((), (), s32[]{:S(2)}) async-start(), calls=%async_computation.5 | async-start | bytes 1474560 | tf_op jit(solution)/shard_map/all_gather | solution.py:74
  7.9 81.2 %all-gather.7.cloned.1.call-start = ((), (), s32[]{:S(2)}) async-start(), calls=%async_computation.4 | async-start | bytes 4423680 | tf_op jit(solution)/shard_map/all_gather | solution.py:73
  8.7 164.0 %all-gather.11.cloned.1.call-start = ((), (), s32[]{:S(2)}) async-start(), calls=%async_computation.6 | async-start | bytes 5898240 | tf_op jit(solution)/shard_map/all_gather | solution.py:75
  9.5 197.3 %all-gather.13.cloned.1.call-start = ((), (), s32[]{:S(2)}) async-start(), calls=%async_computation.7 | async-start | bytes 5898240 | tf_op jit(solution)/shard_map/all_gather | solution.py:76
  10.0 366.1 %reduce-scatter.7.cloned.1.call-start = ((), (), s32[]{:S(2)}) async-start(), calls=%async_computation.10 | async-start | bytes 1474560 | tf_op jit(solution)/shard_map/reduce_scatter | solution.py:271
  98.0 9.0 %collective-permute-start.1 = (bf16[1,128,12,64]{1,3,2,0:T(8,128)(2,1)S(1)}, bf16[1,128,12,64]{1,3,2,0:T(8,128)(2,1)S(1)}, u32[]{:S(2)}, u32[]{:S(2)}) collective-permute-start(bf16[1,128,12,64]{1,3,2,0:T(8,128)(2,1)S(1)} %get-tuple-element.1113), channel_id=1, source_target_pairs={{0,1},{1,2},{2,3},{3,4},{4,5},{5,6},{6,7},{7,0},{8,9},{9,10},{10,1... | collective-permute-start | bytes 589832 | tf_op jit(solution)/shard_map/while/body/eval_jaxpr/ppermute | solution.py:15
  110.0 9.0 %collective-permute-start.1 = (bf16[1,128,12,64]{1,3,2,0:T(8,128)(2,1)S(1)}, bf16[1,128,12,64]{1,3,2,0:T(8,128)(2,1)S(1)}, u32[]{:S(2)}, u32[]{:S(2)}) collective-permute-start(bf16[1,128,12,64]{1,3,2,0:T(8,128)(2,1)S(1)} %get-tuple-element.1113), channel_id=1, source_target_pairs={{0,1},{1,2},{2,3},{3,4},{4,5},{5,6},{6,7},{7,0},{8,9},{9,10},{10,1... | collective-permute-start | bytes 589832 | tf_op jit(solution)/shard_map/while/body/eval_jaxpr/ppermute | solution.py:15
  122.0 9.0 %collective-permute-start.1 = (bf16[1,128,12,64]{1,3,2,0:T(8,128)(2,1)S(1)}, bf16[1,128,12,64]{1,3,2,0:T(8,128)(2,1)S(1)}, u32[]{:S(2)}, u32[]{:S(2)}) collective-permute-start(bf16[1,128,12,64]{1,3,2,0:T(8,128)(2,1)S(1)} %get-tuple-element.1113), channel_id=1, source_target_pairs={{0,1},{1,2},{2,3},{3,4},{4,5},{5,6},{6,7},{7,0},{8,9},{9,10},{10,1... | collective-permute-start | bytes 589832 | tf_op jit(solution)/shard_map/while/body/eval_jaxpr/ppermute | solution.py:15
  131.1 9.0 %collective-permute-start.1 = (bf16[1,128,12,64]{1,3,2,0:T(8,128)(2,1)S(1)}, bf16[1,128,12,64]{1,3,2,0:T(8,128)(2,1)S(1)}, u32[]{:S(2)}, u32[]{:S(2)}) collective-permute-start(bf16[1,128,12,64]{1,3,2,0:T(8,128)(2,1)S(1)} %get-tuple-element.1113), channel_id=1, source_target_pairs={{0,1},{1,2},{2,3},{3,4},{4,5},{5,6},{6,7},{7,0},{8,9},{9,10},{10,1... | collective-permute-start | bytes 589832 | tf_op jit(solution)/shard_map/while/body/eval_jaxpr/ppermute | solution.py:15
  140.2 9.0 %collective-permute-start.1 = (bf16[1,128,12,64]{1,3,2,0:T(8,128)(2,1)S(1)}, bf16[1,128,12,64]{1,3,2,0:T(8,128)(2,1)S(1)}, u32[]{:S(2)}, u32[]{:S(2)}) collective-permute-start(bf16[1,128,12,64]{1,3,2,0:T(8,128)(2,1)S(1)} %get-tuple-element.1113), channel_id=1, source_target_pairs={{0,1},{1,2},{2,3},{3,4},{4,5},{5,6},{6,7},{7,0},{8,9},{9,10},{10,1... | collective-permute-start | bytes 589832 | tf_op jit(solution)/shard_map/while/body/eval_jaxpr/ppermute | solution.py:15
  149.3 9.0 %collective-permute-start.1 = (bf16[1,128,12,64]{1,3,2,0:T(8,128)(2,1)S(1)}, bf16[1,128,12,64]{1,3,2,0:T(8,128)(2,1)S(1)}, u32[]{:S(2)}, u32[]{:S(2)}) collective-permute-start(bf16[1,128,12,64]{1,3,2,0:T(8,128)(2,1)S(1)} %get-tuple-element.1113), channel_id=1, source_target_pairs={{0,1},{1,2},{2,3},{3,4},{4,5},{5,6},{6,7},{7,0},{8,9},{9,10},{10,1... | collective-permute-start | bytes 589832 | tf_op jit(solution)/shard_map/while/body/eval_jaxpr/ppermute | solution.py:15
  161.3 9.0 %collective-permute-start.1 = (bf16[1,128,12,64]{1,3,2,0:T(8,128)(2,1)S(1)}, bf16[1,128,12,64]{1,3,2,0:T(8,128)(2,1)S(1)}, u32[]{:S(2)}, u32[]{:S(2)}) collective-permute-start(bf16[1,128,12,64]{1,3,2,0:T(8,128)(2,1)S(1)} %get-tuple-element.1113), channel_id=1, source_target_pairs={{0,1},{1,2},{2,3},{3,4},{4,5},{5,6},{6,7},{7,0},{8,9},{9,10},{10,1... | collective-permute-start | bytes 589832 | tf_op jit(solution)/shard_map/while/body/eval_jaxpr/ppermute | solution.py:15
  172.6 203.6 %reduce-scatter.9.cloned.1.call-start = ((), (), s32[]{:S(2)}) async-start(), calls=%async_computation.11 | async-start | bytes 5898240 | tf_op jit(solution)/shard_map/reduce_scatter | solution.py:274
  216.9 159.3 %reduce-scatter.11.cloned.1.call-start = ((), (), s32[]{:S(2)}) async-start(), calls=%async_computation.12 | async-start | bytes 5898240 | tf_op jit(solution)/shard_map/reduce_scatter | solution.py:277
  220.6 411.3 %all-gather.15.cloned.1.call-start = ((), (), s32[]{:S(2)}) async-start(), calls=%async_computation.9 | async-start | bytes 31850496 | tf_op jit(solution)/shard_map/all_gather | solution.py:256
  224.6 9.1 %collective-permute-start.7 = (bf16[1,128,12,64]{1,3,2,0:T(8,128)(2,1)S(1)}, bf16[1,128,12,64]{1,3,2,0:T(8,128)(2,1)}, u32[]{:S(2)}, u32[]{:S(2)}) collective-permute-start(bf16[1,128,12,64]{1,3,2,0:T(8,128)(2,1)S(1)} %convert_element_type.293), channel_id=1, source_target_pairs={{0,1},{1,2},{2,3},{3,4},{4,5},{5,6},{6,7},{7,0},{8,9},{9,10},{10,1... | collective-permute-start | bytes 589832 | tf_op jit(solution)/shard_map/ppermute | solution.py:15
  234.7 9.0 %collective-permute-start.3 = (bf16[1,128,12,64]{1,3,2,0:T(8,128)(2,1)S(1)}, bf16[1,128,12,64]{1,3,2,0:T(8,128)(2,1)S(1)}, u32[]{:S(2)}, u32[]{:S(2)}) collective-permute-start(bf16[1,128,12,64]{1,3,2,0:T(8,128)(2,1)S(1)} %get-tuple-element.1171), channel_id=1, source_target_pairs={{0,1},{1,2},{2,3},{3,4},{4,5},{5,6},{6,7},{7,0},{8,9},{9,10},{10,1... | collective-permute-start | bytes 589832 | tf_op jit(solution)/shard_map/while/body/eval_jaxpr/ppermute | solution.py:15
  256.1 9.0 %collective-permute-start.3 = (bf16[1,128,12,64]{1,3,2,0:T(8,128)(2,1)S(1)}, bf16[1,128,12,64]{1,3,2,0:T(8,128)(2,1)S(1)}, u32[]{:S(2)}, u32[]{:S(2)}) collective-permute-start(bf16[1,128,12,64]{1,3,2,0:T(8,128)(2,1)S(1)} %get-tuple-element.1171), channel_id=1, source_target_pairs={{0,1},{1,2},{2,3},{3,4},{4,5},{5,6},{6,7},{7,0},{8,9},{9,10},{10,1... | collective-permute-start | bytes 589832 | tf_op jit(solution)/shard_map/while/body/eval_jaxpr/ppermute | solution.py:15
  277.5 9.0 %collective-permute-start.3 = (bf16[1,128,12,64]{1,3,2,0:T(8,128)(2,1)S(1)}, bf16[1,128,12,64]{1,3,2,0:T(8,128)(2,1)S(1)}, u32[]{:S(2)}, u32[]{:S(2)}) collective-permute-start(bf16[1,128,12,64]{1,3,2,0:T(8,128)(2,1)S(1)} %get-tuple-element.1171), channel_id=1, source_target_pairs={{0,1},{1,2},{2,3},{3,4},{4,5},{5,6},{6,7},{7,0},{8,9},{9,10},{10,1... | collective-permute-start | bytes 589832 | tf_op jit(solution)/shard_map/while/body/eval_jaxpr/ppermute | solution.py:15
  295.7 9.0 %collective-permute-start.3 = (bf16[1,128,12,64]{1,3,2,0:T(8,128)(2,1)S(1)}, bf16[1,128,12,64]{1,3,2,0:T(8,128)(2,1)S(1)}, u32[]{:S(2)}, u32[]{:S(2)}) collective-permute-start(bf16[1,128,12,64]{1,3,2,0:T(8,128)(2,1)S(1)} %get-tuple-element.1171), channel_id=1, source_target_pairs={{0,1},{1,2},{2,3},{3,4},{4,5},{5,6},{6,7},{7,0},{8,9},{9,10},{10,1... | collective-permute-start | bytes 589832 | tf_op jit(solution)/shard_map/while/body/eval_jaxpr/ppermute | solution.py:15
  313.9 9.0 %collective-permute-start.3 = (bf16[1,128,12,64]{1,3,2,0:T(8,128)(2,1)S(1)}, bf16[1,128,12,64]{1,3,2,0:T(8,128)(2,1)S(1)}, u32[]{:S(2)}, u32[]{:S(2)}) collective-permute-start(bf16[1,128,12,64]{1,3,2,0:T(8,128)(2,1)S(1)} %get-tuple-element.1171), channel_id=1, source_target_pairs={{0,1},{1,2},{2,3},{3,4},{4,5},{5,6},{6,7},{7,0},{8,9},{9,10},{10,1... | collective-permute-start | bytes 589832 | tf_op jit(solution)/shard_map/while/body/eval_jaxpr/ppermute | solution.py:15
  332.1 9.0 %collective-permute-start.3 = (bf16[1,128,12,64]{1,3,2,0:T(8,128)(2,1)S(1)}, bf16[1,128,12,64]{1,3,2,0:T(8,128)(2,1)S(1)}, u32[]{:S(2)}, u32[]{:S(2)}) collective-permute-start(bf16[1,128,12,64]{1,3,2,0:T(8,128)(2,1)S(1)} %get-tuple-element.1171), channel_id=1, source_target_pairs={{0,1},{1,2},{2,3},{3,4},{4,5},{5,6},{6,7},{7,0},{8,9},{9,10},{10,1... | collective-permute-start | bytes 589832 | tf_op jit(solution)/shard_map/while/body/eval_jaxpr/ppermute | solution.py:15
  376.1 327.9 %all-reduce.11.cloned.1.call-start = ((), (), s32[]{:S(2)}) async-start(), calls=%async_computation.13 | async-start | bytes 5308416 | tf_op jit(solution)/shard_map/psum | solution.py:257
  376.8 374.8 %reduce-scatter.5.cloned.1.call-start = ((), (), s32[]{:S(2)}) async-start(), calls=%async_computation.8 | async-start | bytes 4423680 | tf_op jit(solution)/shard_map/reduce_scatter | solution.py:268
  (58 other events, 1055.3 us)
Sparse Core Ops, SparseCore 0:
  9.8 30.2 all-gather.8
  42.0 47.1 all-gather.6
  91.0 56.9 all-gather.10
  149.7 56.9 all-gather.12
  210.0 28.6 reduce-scatter.6
  241.6 56.9 reduce-scatter.8
  301.6 56.9 reduce-scatter.10
  376.2 255.7 all-gather.14
  634.6 67.5 all-reduce.10
  705.0 46.5 reduce-scatter.4
